TPU v7x, 32 devices: a whole 2x2x4 slice. The times are simulated.
32 devices in a mesh: ctx: 32 (over z, y, x, core), head: 1.
Axes of the slice: x: 2, y: 2, z: 4, core: 2. Of those that a mesh axis runs over, the one named last changes fastest.
Arguments:
- queries: bfloat16 [6144, 4096], P('ctx', 'head'), may hold values from -6 to 6
- keys: bfloat16 [6144, 1024], P('ctx', 'head'), may hold values from -6 to 6
- values: bfloat16 [6144, 1024], P('ctx', 'head'), may hold values from -6 to 6
- retrieval: int32 [32], replicated, may hold values 0 or 1
- spans: int32 [2, 32], replicated, may hold values from 64 to 4096, as said below
- out_weight: bfloat16 [4096, 4096], P(None, 'head'), may hold values from -0.09375 to 0.09375
Outputs:
- layer_out: bfloat16 [6144, 4096], P('ctx', 'head')
Inputs may be any that keep to these rules, and one draw needn't show every extreme that they name: `spans`: row 0 lies within 64 to 128, row 1 within 2048 to 4096; some head has exactly 128 sink tokens and some head exactly 4096 recent tokens.
All inputs are finite; a program needn't handle non-finite values.
Results may differ from a plain program's by a relative error of at most 0.0075.
Values may be sent and summed in bfloat16 or wider, within the bound.
A program may use at most 192 MiB of HBM per device.

v0:
```python
import jax
import jax.numpy as jnp
from jax import lax
from jax.sharding import PartitionSpec as P

HD = 128


def body(queries, keys, values, retrieval, spans, out_weight):
    row_count = queries.shape[0]
    half_rows = row_count // 2
    local_heads = queries.shape[1] // HD
    kv_heads = keys.shape[1] // HD
    group_size = local_heads // kv_heads
    scale = HD ** (-0.5)
    head_first = lax.axis_index("head") * local_heads
    retrieval_heads = (
        lax.dynamic_slice_in_dim(retrieval, head_first, local_heads).reshape(kv_heads, group_size)
        > 0
    )
    sink_sizes = lax.dynamic_slice_in_dim(spans[0], head_first, local_heads).reshape(
        kv_heads, group_size
    )
    window_sizes = lax.dynamic_slice_in_dim(spans[1], head_first, local_heads).reshape(
        kv_heads, group_size
    )
    cycle_index = lax.axis_index("ctx")
    near_queries = queries[:half_rows]
    far_queries = queries[half_rows:]
    near_pos = cycle_index * row_count + jnp.arange(half_rows, dtype=jnp.int32)
    far_pos = cycle_index * row_count + half_rows + jnp.arange(half_rows, dtype=jnp.int32)
    near_heads = near_queries.reshape(half_rows, kv_heads, group_size, HD)
    far_heads = far_queries.reshape(half_rows, kv_heads, group_size, HD)

    def update(state, query_heads, query_pos, key_heads, value_heads, key_pos):
        maxima, totals, accum = state
        scores = (
            jnp.einsum("qgjd,kgd->qgjk", query_heads, key_heads, preferred_element_type=jnp.float32)
            * scale
        )
        gap = query_pos[:, None] - key_pos[None, :]
        reach = retrieval_heads[None, :, :, None] | (
            key_pos[None, None, None, :] < sink_sizes[None, :, :, None]
        )
        reach = reach | (gap[:, None, None, :] < window_sizes[None, :, :, None])
        allowed = (gap >= 0)[:, None, None, :] & reach
        masked = jnp.where(allowed, scores, -1e30)
        fresh = jnp.maximum(maxima, jnp.max(masked, axis=-1))
        weights = jnp.where(allowed, jnp.exp(masked - fresh[..., None]), 0.0)
        totals = jnp.sum(weights, axis=-1)
        added = jnp.einsum(
            "qgjk,kgd->qgjd",
            weights.astype(jnp.bfloat16),
            value_heads,
            preferred_element_type=jnp.float32,
        )
        accum = added
        return (fresh, totals, accum)

    def visit(state, query_heads, query_pos, key_heads, value_heads, key_pos, offset):

        def active(held):
            return update(held, query_heads, query_pos, key_heads, value_heads, key_pos)

        def skipped(held):
            return held

        return lax.cond(offset <= query_pos[-1], active, skipped, state)

    start_state = (
        jnp.full((half_rows, kv_heads, group_size), -1e30, jnp.float32),
        jnp.zeros((half_rows, kv_heads, group_size), jnp.float32),
        jnp.zeros((half_rows, kv_heads, group_size, HD), jnp.float32),
    )
    pieces = (
        lax.all_gather(keys, "ctx", axis=0, tiled=True),
        lax.all_gather(values, "ctx", axis=0, tiled=True),
    )
    offset = jnp.int32(0)
    key_rows = pieces[0].shape[0]
    key_heads = pieces[0].reshape(key_rows, kv_heads, HD)
    value_heads = pieces[1].reshape(key_rows, kv_heads, HD)
    key_pos = jnp.arange(key_rows, dtype=jnp.int32)
    near_state = visit(start_state, near_heads, near_pos, key_heads, value_heads, key_pos, offset)
    far_state = visit(start_state, far_heads, far_pos, key_heads, value_heads, key_pos, offset)
    near_state, far_state = (near_state, far_state)

    def finish(state):
        return (
            (state[2] / state[1][..., None])
            .reshape(half_rows, local_heads * HD)
            .astype(jnp.bfloat16)
        )

    near_attended = finish(near_state)
    far_attended = finish(far_state)
    attended = jnp.concatenate([near_attended, far_attended], axis=0)
    features = lax.all_gather(attended, "head", axis=1, tiled=True)
    projected = jnp.dot(features, out_weight, preferred_element_type=jnp.float32)
    return projected.astype(jnp.bfloat16)


def solution(mesh):
    in_specs = (P("ctx", "head"), P("ctx", "head"), P("ctx", "head"), P(), P(), P(None, "head"))
    out_specs = P("ctx", "head")
    return jax.shard_map(body, mesh=mesh, in_specs=in_specs, out_specs=out_specs, check_vma=False)
```

profile of v0, /device:TPU:29, one launch (start us, length us, event | category | flops | bytes accessed | tf_op | source)
XLA Modules:
  0.0 471.9 jit_solution(1809647474993605472)
XLA Ops:
  6.5 0.7 all-gather.3.cloned.1.call-update
  7.3 0.7 all-gather.5.cloned.1.call-update
  8.0 0.6 slice.20
  9.3 0.6 slice.23
  10.5 0.7 broadcast_compare_fusion.2
  11.3 0.8 slice_bitcast_fusion
  12.0 93.3 %all-gather.3.cloned.1.call-done = bf16[6144,1024]{1,0:T(8,128)(2,1)} async-done(((bf16[192,1024]{1,0:T(8,128)(2,1)}), bf16[6144,1024]{1,0:T(8,128)(2,1)}) %all-gather.3.cloned.1.call-update) | async-done | bytes 12582928 | tf_op jit(solution)/shard_map/all_gather | solution.py:76
  105.3 16.8 %copy.23 = bf16[6144,1024]{0,1:T(8,128)(2,1)} copy(bf16[6144,1024]{1,0:T(8,128)(2,1)} %all-gather.3.cloned.1.call-done) | data formatting | bytes 25165824 | tf_op jit(solution)/shard_map/all_gather | solution.py:76
  122.1 79.9 %all-gather.5.cloned.1.call-done = bf16[6144,1024]{1,0:T(8,128)(2,1)} async-done(((bf16[192,1024]{1,0:T(8,128)(2,1)}), bf16[6144,1024]{1,0:T(8,128)(2,1)}) %all-gather.5.cloned.1.call-update) | async-done | bytes 12582928 | tf_op jit(solution)/shard_map/all_gather | solution.py:77
  202.0 16.7 %copy.24 = bf16[6144,1024]{0,1:T(8,128)(2,1)} copy(bf16[6144,1024]{1,0:T(8,128)(2,1)} %all-gather.5.cloned.1.call-done) | data formatting | bytes 25165824 | tf_op jit(solution)/shard_map/all_gather | solution.py:77
  218.7 111.5 %conditional.2 = (f32[96,8,4]{0,2,1:T(4,128)S(1)}, f32[96,8,4,128]{3,0,2,1:T(8,128)}) conditional(s32[]{:T(128)} %bitcast.8, () %tuple.21, (s32[96]{0:T(128)S(1)}, s32[6144]{0:T(1024)S(1)}, pred[8,4]{1,0:T(8,128)(4,1)S(1)}, s32[6144]{0:T(1024)S(1)}, s32[32]{0:T(128)S(1)}, /*index=5*/s32[32]{0:T(128)S(1)}, bf16[192,4096]{1,0:T(8,128)(2,1)S(1)}, ...), branch_computations={%region_0.0_spmd, %region_1.4_spmd} | conditional | flops 10081072128 | bytes 269895488 | solution.py:68
  218.9 0.3 compare_or_fusion
  219.2 0.4 broadcast_compare_fusion
  219.7 1.4 reshape.145
  221.4 34.7 %fusion = (f32[96,8,4]{0,2,1:T(4,128)S(1)}, f32[8,6144,96,4]{1,2,3,0:T(8,128)}) fusion(s32[8,4]{1,0:T(8,128)S(1)} %lt.62, s32[96,6144]{1,0:T(8,128)S(1)} %broadcast_subtract_fusion, pred[8,4,6144]{2,1,0:T(4,128)(4,1)S(1)} %compare_or_fusion, pred[96,6144]{1,0:T(8,128)(4,1)S(1)} %broadcast_compare_fusion, bf16[96,8,4,128]{3,2,1,0:T(4,128)(2,1)} %reshape.145, ...), kind=kOutput, calls=%fused_computation.3 | convolution fusion | flops 4945081344 | bytes 92024960 | tf_op jit(solution)/shard_map/cond/branch_1_fun/qgjd,kgd->qgjk/dot_general | solution.py:38
  256.2 35.2 %fusion.10 = f32[96,8,4,128]{3,0,2,1:T(8,128)} fusion(bf16[6144,8,128]{0,2,1:T(8,128)(2,1)} %get-tuple-element.95, f32[8,6144,96,4]{1,2,3,0:T(8,128)} %get-tuple-element.106, f32[96,8,4]{0,2,1:T(4,128)S(1)} %broadcast_maximum_fusion, s32[8,4]{1,0:T(8,128)S(1)} %lt.62, s32[96,6144]{1,0:T(8,128)S(1)} %broadcast_subtract_fusion, ...), kind=kOutput, calls=%fused_computation.12 | convolution fusion | flops 4982833152 | bytes 92811392 | tf_op jit(solution)/shard_map/cond/branch_1_fun/qgjk,kgd->qgjd/dot_general | solution.py:51
  291.4 38.6 %fusion.2 = f32[96,8,4]{0,2,1:T(4,128)S(1)} fusion(f32[8,6144,96,4]{1,2,3,0:T(8,128)} %get-tuple-element.106, f32[96,8,4]{0,2,1:T(4,128)S(1)} %broadcast_maximum_fusion, s32[8,4]{1,0:T(8,128)S(1)} %lt.62, s32[96,6144]{1,0:T(8,128)S(1)} %broadcast_subtract_fusion, pred[8,4,6144]{2,1,0:T(4,128)(4,1)S(1)} %compare_or_fusion, ...), kind=kLoop, calls=%fused_computation.5 | loop fusion | flops 150991872 | bytes 78667904 | tf_op jit(solution)/shard_map/cond/branch_1_fun/reduce_sum | solution.py:50
  330.2 1.9 divide_convert_fusion.1
  332.1 0.4 copy.27
  332.5 1.5 convert_element_type.36
  334.0 112.8 %conditional.3 = (f32[96,8,4]{0,2,1:T(4,128)S(1)}, f32[96,8,4,128]{3,0,2,1:T(8,128)}) conditional(s32[]{:T(128)} %bitcast.13, () %tuple.23, (s32[96]{0:T(128)S(1)}, s32[6144]{0:T(1024)S(1)}, pred[8,4]{1,0:T(8,128)(4,1)S(1)}, s32[6144]{0:T(1024)S(1)}, s32[32]{0:T(128)S(1)}, /*index=5*/s32[32]{0:T(128)S(1)}, bf16[192,4096]{1,0:T(8,128)(2,1)}, ...), branch_computations={%region_4.5_spmd, %region_5.8_spmd} | conditional | flops 10081072128 | bytes 269895488 | solution.py:68
  334.1 0.3 compare_or_fusion.1
  334.5 0.4 broadcast_compare_fusion.1
  334.9 1.2 slice.15
  336.1 1.4 reshape.146
  337.8 34.8 %fusion.19 = (f32[96,8,4]{0,2,1:T(4,128)S(1)}, f32[8,6144,96,4]{1,2,3,0:T(8,128)}) fusion(s32[8,4]{1,0:T(8,128)S(1)} %lt.70, s32[96,6144]{1,0:T(8,128)S(1)} %broadcast_subtract_fusion.1, pred[8,4,6144]{2,1,0:T(4,128)(4,1)S(1)} %compare_or_fusion.1, pred[96,6144]{1,0:T(8,128)(4,1)S(1)} %broadcast_compare_fusion.1, bf16[96,8,4,128]{3,2,1,0:T(4,128)(2,1)} %reshape.146, ...), kind=kOutput, calls=%fused_computation.24 | convolution fusion | flops 4945081344 | bytes 92024960 | tf_op jit(solution)/shard_map/cond/branch_1_fun/qgjd,kgd->qgjk/dot_general | solution.py:38
  372.6 35.2 %fusion.29 = f32[96,8,4,128]{3,0,2,1:T(8,128)} fusion(bf16[6144,8,128]{0,2,1:T(8,128)(2,1)} %get-tuple-element.104, f32[8,6144,96,4]{1,2,3,0:T(8,128)} %get-tuple-element.108, f32[96,8,4]{0,2,1:T(4,128)S(1)} %broadcast_maximum_fusion.1, s32[8,4]{1,0:T(8,128)S(1)} %lt.70, s32[96,6144]{1,0:T(8,128)S(1)} %broadcast_subtract_fusion.1, ...), kind=kOutput, calls=%fused_computation.33 | convolution fusion | flops 4982833152 | bytes 92811392 | tf_op jit(solution)/shard_map/cond/branch_1_fun/qgjk,kgd->qgjd/dot_general | solution.py:51
  407.9 38.6 %fusion.21 = f32[96,8,4]{0,2,1:T(4,128)S(1)} fusion(f32[8,6144,96,4]{1,2,3,0:T(8,128)} %get-tuple-element.108, f32[96,8,4]{0,2,1:T(4,128)S(1)} %broadcast_maximum_fusion.1, s32[8,4]{1,0:T(8,128)S(1)} %lt.70, s32[96,6144]{1,0:T(8,128)S(1)} %broadcast_subtract_fusion.1, pred[8,4,6144]{2,1,0:T(4,128)(4,1)S(1)} %compare_or_fusion.1, ...), kind=kLoop, calls=%fused_computation.26 | loop fusion | flops 150991872 | bytes 78667904 | tf_op jit(solution)/shard_map/cond/branch_1_fun/reduce_sum | solution.py:50
  446.8 1.9 divide_convert_fusion
  448.7 0.4 copy.30
  449.1 0.6 convert_element_type.40
  449.7 15.4 %convolution_convert_fusion = bf16[192,4096]{1,0:T(8,128)(2,1)} fusion(bf16[4096,4096]{1,0:T(8,128)(2,1)} %param.15, bf16[96,4096]{1,0:T(8,128)(2,1)S(1)} %convert_element_type.40, bf16[96,4096]{1,0:T(8,128)(2,1)} %convert_element_type.36), kind=kOutput, calls=%fused_computation.42 | convolution fusion | flops 6446383104 | bytes 36700160 | tf_op jit(solution)/shard_map/dot_general | solution.py:99
  (22 shorter events, 1.0 us)
Async XLA Ops:
  6.5 98.8 %all-gather.3.cloned.1.call-start = ((), (), s32[]{:S(2)}) async-start(), calls=%async_computation | async-start | bytes 12976128 | tf_op jit(solution)/shard_map/all_gather | solution.py:76
  7.3 194.7 %all-gather.5.cloned.1.call-start = ((), (), s32[]{:S(2)}) async-start(), calls=%async_computation.1 | async-start | bytes 12976128 | tf_op jit(solution)/shard_map/all_gather | solution.py:77
  9.3 1.2 copy-start.1
  122.1 96.6 %copy-start = (bf16[192,4096]{1,0:T(8,128)(2,1)S(1)}, bf16[192,4096]{1,0:T(8,128)(2,1)}, u32[]{:S(2)}) copy-start(bf16[192,4096]{1,0:T(8,128)(2,1)} %param.10) | copy-start | bytes 4718596
  218.7 115.3 %copy-start.2 = (s32[96]{0:T(128)S(1)}, s32[96]{0:T(128)}, u32[]{:S(2)}) copy-start(s32[96]{0:T(128)} %copy-done.1) | copy-start | bytes 1156
Sparse Core Ops, SparseCore 0:
  10.2 95.0 all-gather.2
  108.2 93.7 all-gather.4
where the time goes:
time: 476 us; the launch traced here: 472 us
  waiting for transfers between devices  175 us (37%)
  matrix products  155 us (33%)
  other arithmetic  83.7 us (18%)
  local copies, waits for them, and re-layouts  42.8 us (9%)
  between operations  14.8 us (3%)
    all_gather x1, waiting for transfers between devices, body(): lax.all_gather(keys, 'ctx', axis=0, tiled=True)  93.3 us
    all_gather x1, waiting for transfers between devices, body(): lax.all_gather(values, 'ctx', axis=0, tiled=True)  79.9 us
    reduce_sum x2, other arithmetic, update(): totals = jnp.sum(weights, axis=-1)  77.2 us
    dot_general x2, matrix products, update(): jnp.einsum('qgjk,kgd->qgjd', weights.astype(jnp.bfloat16), value_heads, p...  70.4 us
    dot_general x2, matrix products, update(): jnp.einsum('qgjd,kgd->qgjk', query_heads, key_heads, preferred_element_ty...  69.5 us
    all_gather x1, local copies, waits for them, and re-layouts, body(): lax.all_gather(keys, 'ctx', axis=0, tiled=True)  16.8 us
    all_gather x1, local copies, waits for them, and re-layouts, body(): lax.all_gather(values, 'ctx', axis=0, tiled=True)  16.7 us
    dot_general x1, matrix products, body(): jnp.dot(features, out_weight, preferred_element_type=jnp.float32)  15.4 us
  transfers between devices with their start and end apart: 2, of which 2 were waited for; matrix products, arithmetic and copies ran while one was open for 4% of the time, Pallas kernels for 0%

commit v1 on v0

v1 whole, which is shorter than its diff:
```python
import functools

import jax
import jax.numpy as jnp
from jax import lax
from jax.experimental import pallas as pl
from jax.experimental.pallas import tpu as pltpu
from jax.sharding import PartitionSpec as P

HD = 128
LOG2E = 1.4426950408889634
MASKED = -1e30
FLOOR = -1e29
FAR = 1 << 29


def attend_kernel(group, block, first_head, meta_ref, pos_ref, q_ref, k_ref, v_ref, o_ref, stacked, peak, total, accum):
    rows = q_ref.shape[0]
    scale = (HD ** -0.5) * LOG2E
    head = first_head + pl.program_id(0) * group
    first_row = pos_ref[0]
    last_row = first_row + rows - 1
    sinks = [meta_ref[0, head + r] for r in range(group)]
    windows = [meta_ref[1, head + r] for r in range(group)]
    widest = functools.reduce(jnp.maximum, windows)
    narrowest = functools.reduce(jnp.minimum, windows)
    most_sink = functools.reduce(jnp.maximum, sinks)

    for r in range(group):
        stacked[r * rows:(r + 1) * rows, :] = q_ref[:, r * HD:(r + 1) * HD]
    peak[...] = jnp.full_like(peak, FLOOR)
    total[...] = jnp.zeros_like(total)
    accum[...] = jnp.zeros_like(accum)

    def step(index, masked):
        start = pl.multiple_of(index * block, block)
        scores = lax.dot_general(
            stacked[...], k_ref[pl.ds(start, block), :], (((1,), (1,)), ((), ())),
            preferred_element_type=jnp.float32,
        )
        if masked:
            key_pos = start + lax.broadcasted_iota(jnp.int32, (rows, block), 1)
            gap = first_row - key_pos + lax.broadcasted_iota(jnp.int32, (rows, block), 0)
            parts = []
            for r in range(group):
                allowed = (gap >= 0) & ((gap < windows[r]) | (key_pos < sinks[r]))
                parts.append(jnp.where(allowed, scores[r * rows:(r + 1) * rows], MASKED))
            scores = jnp.concatenate(parts, axis=0)
        held = peak[...]
        fresh = jnp.maximum(held, jnp.max(scores, axis=-1, keepdims=True))
        peak[...] = fresh
        shrink = jnp.exp2((held - fresh) * scale)
        weights = jnp.exp2((scores - jnp.tile(fresh, (1, block // HD))) * scale)
        added = weights[:, :HD]
        for c in range(1, block // HD):
            added = added + weights[:, c * HD:(c + 1) * HD]
        total[...] = total[...] * shrink + added
        accum[...] = accum[...] * shrink + jnp.dot(
            weights.astype(jnp.bfloat16), v_ref[pl.ds(start, block), :],
            preferred_element_type=jnp.float32,
        )

    low = jnp.maximum(first_row - widest + 1, 0) // block
    high = last_row // block + 1
    full_low = jnp.minimum((jnp.maximum(last_row - narrowest + 1, 0) + block - 1) // block, high)
    full_high = jnp.maximum((first_row + 1) // block, full_low)
    sink_blocks = jnp.minimum((most_sink + block - 1) // block, low)
    count_low = jnp.maximum(full_low - low, 0)
    masked_count = sink_blocks + count_low + (high - full_high)

    def masked_step(i, carry):
        near = i - sink_blocks
        index = jnp.where(
            near < 0, i, jnp.where(near < count_low, low + near, full_high + near - count_low)
        )
        step(index, True)
        return carry

    def full_step(i, carry):
        step(i, False)
        return carry

    lax.fori_loop(0, masked_count, masked_step, 0)
    lax.fori_loop(full_low, full_high, full_step, 0)
    mixed = accum[...] / jnp.sum(total[...], axis=-1, keepdims=True)
    for r in range(group):
        o_ref[:, r * HD:(r + 1) * HD] = mixed[r * rows:(r + 1) * rows].astype(jnp.bfloat16)


def attend(queries, gathered, meta, position, group, first_kv, kv_count):
    rows = queries.shape[0]
    seq = gathered.shape[0]
    block = 512 if seq % 512 == 0 else HD
    smem = pl.BlockSpec(memory_space=pltpu.SMEM)
    return pl.pallas_call(
        functools.partial(attend_kernel, group, block, first_kv * group),
        grid=(kv_count,),
        out_shape=jax.ShapeDtypeStruct((rows, kv_count * group * HD), jnp.bfloat16),
        in_specs=[
            smem,
            smem,
            pl.BlockSpec((rows, group * HD), lambda g: (0, first_kv + g)),
            pl.BlockSpec((seq, HD), lambda g: (0, g)),
            pl.BlockSpec((seq, HD), lambda g: (0, kv_count + g)),
        ],
        out_specs=pl.BlockSpec((rows, group * HD), lambda g: (0, g)),
        scratch_shapes=[
            pltpu.VMEM((group * rows, HD), jnp.bfloat16),
            pltpu.VMEM((group * rows, HD), jnp.float32),
            pltpu.VMEM((group * rows, HD), jnp.float32),
            pltpu.VMEM((group * rows, HD), jnp.float32),
        ],
        compiler_params=pltpu.CompilerParams(dimension_semantics=("arbitrary",)),
        cost_estimate=pl.CostEstimate(
            flops=8 * kv_count * group * rows * seq * HD,
            bytes_accessed=2 * kv_count * seq * HD * 2,
            transcendentals=kv_count * group * rows * seq,
        ),
    )(meta, position, queries, gathered, gathered)


def body(queries, keys, values, retrieval, spans, out_weight):
    rows = queries.shape[0]
    local_heads = queries.shape[1] // HD
    kv_heads = keys.shape[1] // HD
    group = local_heads // kv_heads
    head_first = lax.axis_index("head") * local_heads
    windows = jnp.where(retrieval > 0, FAR, spans[1])
    meta = lax.dynamic_slice_in_dim(jnp.stack([spans[0], windows]), head_first, local_heads, axis=1)
    position = (lax.axis_index("ctx") * rows).reshape(1).astype(jnp.int32)
    step = 2 if kv_heads % 2 == 0 else 1
    gathered = []
    for g in range(0, kv_heads, step):
        columns = slice(g * HD, (g + step) * HD)
        own = jnp.concatenate([keys[:, columns], values[:, columns]], axis=1)
        gathered.append(lax.all_gather(own, "ctx", axis=0, tiled=True))
    pieces = [
        attend(queries, gathered[i], meta, position, group, g, step)
        for i, g in enumerate(range(0, kv_heads, step))
    ]
    attended = jnp.concatenate(pieces, axis=1)
    features = lax.all_gather(attended, "head", axis=1, tiled=True)
    projected = jnp.dot(features, out_weight, preferred_element_type=jnp.float32)
    return projected.astype(jnp.bfloat16)


def solution(mesh):
    in_specs = (P("ctx", "head"), P("ctx", "head"), P("ctx", "head"), P(), P(), P(None, "head"))
    out_specs = P("ctx", "head")
    return jax.shard_map(body, mesh=mesh, in_specs=in_specs, out_specs=out_specs, check_vma=False)
```

time: 476 us -> 335 us (0.70); the launches traced: 472 us -> 336 us
  matrix products: 155 us -> 15.3 us
  Pallas kernels: 0 us -> 93 us
  other arithmetic: 83.7 us -> 3.33 us
  local copies, waits for them, and re-layouts: 42.8 us -> 1.32 us
  waiting for transfers between devices: 175 us -> 210 us
    dot_general x4 -> x0, matrix products: 140 us -> none  [the longest x2 70.4 us: update(): jnp.einsum('qgjk,kgd->qgjd', weights.astype(jnp.bfloat16), value_heads, p...]
    pallas_call x0 -> x4, Pallas kernels: none -> 93 us  [attend(): pl.pallas_call(functools.partial(attend_kernel, group, block, first_kv *...]
    reduce_sum x2 -> x0, other arithmetic: 77.2 us -> none  [update(): totals = jnp.sum(weights, axis=-1)]
    all_gather x2 -> x4, waiting for transfers between devices: 173 us -> 210 us  [body(): gathered.append(lax.all_gather(own, 'ctx', axis=0, tiled=True))]
    all_gather x2 -> x0, local copies, waits for them, and re-layouts: 33.4 us -> none  [the longest x1 16.8 us: body(): lax.all_gather(keys, 'ctx', axis=0, tiled=True)]
  transfers between devices with their start and end apart: 2 -> 4, of which waited for: 2 -> 4; matrix products, arithmetic and copies ran while one was open for 4% -> 1% of each run, Pallas kernels for 0% -> 21%
where the time goes in v1:
time: 335 us; the launch traced here: 336 us
  waiting for transfers between devices  210 us (63%)
  Pallas kernels  93 us (28%)
  matrix products  15.3 us (5%)
  between operations  13.2 us (4%)
    all_gather x4, waiting for transfers between devices, body(): gathered.append(lax.all_gather(own, 'ctx', axis=0, tiled=True))  210 us
    pallas_call x4, Pallas kernels, attend(): pl.pallas_call(functools.partial(attend_kernel, group, block, first_kv *...  93 us
    dot_general x1, matrix products, body(): jnp.dot(features, out_weight, preferred_element_type=jnp.float32)  15.3 us
  transfers between devices with their start and end apart: 4, of which 4 were waited for; matrix products, arithmetic and copies ran while one was open for 1% of the time, Pallas kernels for 21%

profile of v1, /device:TPU:29, one launch (start us, length us, event | category | flops | bytes accessed | tf_op | source)
XLA Modules:
  0.0 336.3 jit_solution(672803603632289413)
XLA Ops:
  6.5 0.0 copy-start
  6.5 0.0 slice-start
  6.5 0.0 copy-start.1
  6.5 0.0 all-gather.5.cloned.1.call-start
  6.5 1.3 fusion.9
  7.8 0.7 pad_maximum_fusion
  8.5 0.0 all-gather.5.cloned.1.call-update
  8.6 0.0 all-gather.7.cloned.1.call-start
  8.6 0.7 pad_maximum_fusion.1
  9.3 0.0 all-gather.7.cloned.1.call-update
  9.3 0.0 all-gather.11.cloned.1.call-start
  9.4 0.7 pad_maximum_fusion.3
  10.1 0.0 all-gather.11.cloned.1.call-update
  10.1 0.0 all-gather.9.cloned.1.call-start
  10.1 0.7 pad_maximum_fusion.2
  10.8 0.0 all-gather.9.cloned.1.call-update
  10.9 0.0 copy-done
  10.9 0.0 copy-done.1
  10.9 0.0 slice-done
  10.9 0.6 pad_add_fusion.meta_ref
  11.5 67.8 %all-gather.5.cloned.1.call-done.k_ref.v_ref = bf16[6144,512]{1,0:T(8,128)(2,1)} async-done(((bf16[192,512]{1,0:T(8,128)(2,1)}), bf16[6144,512]{1,0:T(8,128)(2,1)}) %all-gather.5.cloned.1.call-update) | async-done | bytes 6291472 | tf_op jit(solution)/shard_map/all_gather | solution.py:136
  79.3 23.7 %shard_map.64 = bf16[192,1024]{1,0:T(8,128)(2,1)} custom-call(s32[2,32]{1,0:T(2,128)} %pad_add_fusion.meta_ref, s32[1]{0:T(128)} %bitcast.2.pos_ref, bf16[192,4096]{1,0:T(8,128)(2,1)} %q_ref.7, bf16[6144,512]{1,0:T(8,128)(2,1)} %all-gather.5.cloned.1.call-done.k_ref.v_ref, bf16[6144,512]{1,0:T(8,128)(2,1)} %all-gather.5.cloned.1.call-done.k_ref.v_ref), custom_call_target="tpu_custom_call" | custom-call | flops 9663676416 | bytes 6291456 | tf_op jit(solution)/shard_map/pallas_call | solution.py:95
  102.9 46.9 %all-gather.7.cloned.1.call-done.k_ref.v_ref = bf16[6144,512]{1,0:T(8,128)(2,1)} async-done(((bf16[192,512]{1,0:T(8,128)(2,1)}), bf16[6144,512]{1,0:T(8,128)(2,1)}) %all-gather.7.cloned.1.call-update) | async-done | bytes 6291472 | tf_op jit(solution)/shard_map/all_gather | solution.py:136
  149.9 21.7 %shard_map.65 = bf16[192,1024]{1,0:T(8,128)(2,1)} custom-call(s32[2,32]{1,0:T(2,128)} %pad_add_fusion.meta_ref, s32[1]{0:T(128)} %bitcast.2.pos_ref, bf16[192,4096]{1,0:T(8,128)(2,1)} %q_ref.7, bf16[6144,512]{1,0:T(8,128)(2,1)} %all-gather.7.cloned.1.call-done.k_ref.v_ref, bf16[6144,512]{1,0:T(8,128)(2,1)} %all-gather.7.cloned.1.call-done.k_ref.v_ref), custom_call_target="tpu_custom_call" | custom-call | flops 9663676416 | bytes 6291456 | tf_op jit(solution)/shard_map/pallas_call | solution.py:95
  171.5 48.9 %all-gather.11.cloned.1.call-done.k_ref.v_ref = bf16[6144,512]{1,0:T(8,128)(2,1)} async-done(((bf16[192,512]{1,0:T(8,128)(2,1)}), bf16[6144,512]{1,0:T(8,128)(2,1)}) %all-gather.11.cloned.1.call-update) | async-done | bytes 6291472 | tf_op jit(solution)/shard_map/all_gather | solution.py:136
  220.4 24.0 %shard_map.67 = bf16[192,1024]{1,0:T(8,128)(2,1)} custom-call(s32[2,32]{1,0:T(2,128)} %pad_add_fusion.meta_ref, s32[1]{0:T(128)} %bitcast.2.pos_ref, bf16[192,4096]{1,0:T(8,128)(2,1)} %q_ref.7, bf16[6144,512]{1,0:T(8,128)(2,1)} %all-gather.11.cloned.1.call-done.k_ref.v_ref, bf16[6144,512]{1,0:T(8,128)(2,1)} %all-gather.11.cloned.1.call-done.k_ref.v_ref), custom_call_target="tpu_custom_call" | custom-call | flops 9663676416 | bytes 6291456 | tf_op jit(solution)/shard_map/pallas_call | solution.py:95
  244.5 46.4 %all-gather.9.cloned.1.call-done.k_ref.v_ref = bf16[6144,512]{1,0:T(8,128)(2,1)} async-done(((bf16[192,512]{1,0:T(8,128)(2,1)}), bf16[6144,512]{1,0:T(8,128)(2,1)}) %all-gather.9.cloned.1.call-update) | async-done | bytes 6291472 | tf_op jit(solution)/shard_map/all_gather | solution.py:136
  290.9 23.6 %shard_map.66 = bf16[192,1024]{1,0:T(8,128)(2,1)} custom-call(s32[2,32]{1,0:T(2,128)} %pad_add_fusion.meta_ref, s32[1]{0:T(128)} %bitcast.2.pos_ref, bf16[192,4096]{1,0:T(8,128)(2,1)} %q_ref.7, bf16[6144,512]{1,0:T(8,128)(2,1)} %all-gather.9.cloned.1.call-done.k_ref.v_ref, bf16[6144,512]{1,0:T(8,128)(2,1)} %all-gather.9.cloned.1.call-done.k_ref.v_ref), custom_call_target="tpu_custom_call" | custom-call | flops 9663676416 | bytes 6291456 | tf_op jit(solution)/shard_map/pallas_call | solution.py:95
  314.5 0.0 copy-done.2
  314.5 0.0 copy-done.3
  314.5 0.0 copy-done.4
  314.5 15.3 %convolution_convert_fusion = bf16[192,4096]{1,0:T(8,128)(2,1)} fusion(bf16[4096,4096]{1,0:T(8,128)(2,1)} %param.11, bf16[192,1024]{1,0:T(8,128)(2,1)S(1)} %copy-done.4, bf16[192,1024]{1,0:T(8,128)(2,1)} %shard_map.66, bf16[192,1024]{1,0:T(8,128)(2,1)S(1)} %copy-done.3, bf16[192,1024]{1,0:T(8,128)(2,1)S(1)} %copy-done.2), kind=kOutput, calls=%fused_computation | convolution fusion | flops 6449528832 | bytes 36700160 | tf_op jit(solution)/shard_map/dot_general | solution.py:143
  (4 shorter events, 0.0 us)
Async XLA Ops:
  6.5 4.3 %copy-start = (s32[2,32]{1,0:T(2,128)S(1)}, s32[2,32]{1,0:T(2,128)}, u32[]{:S(2)}) copy-start(s32[2,32]{1,0:T(2,128)} %param.10) | copy-start | bytes 772
  6.5 4.4 %slice-start = ((s32[2,32]{1,0:T(2,128)}), s32[1,32]{1,0:T(1,128)S(1)}, s32[]{:S(2)}) async-start(s32[2,32]{1,0:T(2,128)} %param.10), calls=%async_computation.4 | async-start | bytes 1024 | tf_op jit(solution)/shard_map/slice | solution.py:129
  6.5 4.3 %copy-start.1 = (s32[32]{0:T(128)S(1)}, s32[32]{0:T(128)}, u32[]{:S(2)}) copy-start(s32[32]{0:T(128)} %param.9) | copy-start | bytes 388
  6.5 72.7 %all-gather.5.cloned.1.call-start = ((), (), s32[]{:S(2)}) async-start(), calls=%async_computation | async-start | bytes 6488064 | tf_op jit(solution)/shard_map/all_gather | solution.py:136
  8.6 141.3 %all-gather.7.cloned.1.call-start = ((), (), s32[]{:S(2)}) async-start(), calls=%async_computation.1 | async-start | bytes 6488064 | tf_op jit(solution)/shard_map/all_gather | solution.py:136
  9.3 211.1 %all-gather.11.cloned.1.call-start = ((), (), s32[]{:S(2)}) async-start(), calls=%async_computation.3 | async-start | bytes 6488064 | tf_op jit(solution)/shard_map/all_gather | solution.py:136
  10.1 280.8 %all-gather.9.cloned.1.call-start = ((), (), s32[]{:S(2)}) async-start(), calls=%async_computation.2 | async-start | bytes 6488064 | tf_op jit(solution)/shard_map/all_gather | solution.py:136
  244.4 70.1 %copy-start.2 = (bf16[192,1024]{1,0:T(8,128)(2,1)S(1)}, bf16[192,1024]{1,0:T(8,128)(2,1)}, u32[]{:S(2)}) copy-start(bf16[192,1024]{1,0:T(8,128)(2,1)} %shard_map.64) | copy-start | bytes 1179652
  244.4 70.1 %copy-start.3 = (bf16[192,1024]{1,0:T(8,128)(2,1)S(1)}, bf16[192,1024]{1,0:T(8,128)(2,1)}, u32[]{:S(2)}) copy-start(bf16[192,1024]{1,0:T(8,128)(2,1)} %shard_map.65) | copy-start | bytes 1179652
  244.4 70.1 %copy-start.4 = (bf16[192,1024]{1,0:T(8,128)(2,1)S(1)}, bf16[192,1024]{1,0:T(8,128)(2,1)}, u32[]{:S(2)}) copy-start(bf16[192,1024]{1,0:T(8,128)(2,1)} %shard_map.67) | copy-start | bytes 1179652
Sparse Core Ops, SparseCore 0:
  10.2 69.0 all-gather.4
  82.1 67.6 all-gather.6
  152.7 67.6 all-gather.10
  223.2 67.6 all-gather.8
